TPU v7x, 32 devices: a whole 2x2x4 slice. The times are simulated.
32 devices in a mesh: study: 2 (over x), ky: 16 (over z, y, core).
Axes of the slice: x: 2, y: 2, z: 4, core: 2. Of those that a mesh axis runs over, the one named last changes fastest.
Arguments:
- kspace: bfloat16 [32, 2, 32, 256, 256], P('study', None, None, 'ky'), parts along dimension 0, may hold values from -6 to 6
- kernel: bfloat16 [2, 768, 64], replicated, may hold values from -0.21875 to 0.21875
- pattern: int32 [32], P('study'), parts along dimension 0, may hold values from 0 to 2
- offsets: int32 [4], replicated, may hold values from -2 to 2
- segment: int32 [256], replicated, may hold values from 0 to 2
- temporal_basis: float32 [5, 16], replicated, may hold values from -1.5 to 1.5
Outputs:
- basis_images: float32 [10, 2, 32, 256, 256], P('study', None, None, 'ky'), parts along dimension 0
There are 2 independent parts, one for each index of `study`. A program takes and returns all parts, laid end to end along the dimension named above; an argument that names none is the same for every part. Nothing has to cross between parts.
All inputs are finite; a program needn't handle non-finite values.
Results may differ from a plain program's by a relative error of at most 0.0003.
Values may be sent and summed in bfloat16 or wider, within the bound.
No kernel may reach another device: no remote copies, remote signals or barrier semaphores. Data moves between devices by JAX's collectives and lax.ppermute only.
A program may use at most 192 MiB of HBM per device.

v0:
```python
import jax
import jax.numpy as jnp
from jax import lax
from jax.sharding import PartitionSpec as P

frame_block = 4


def padded_2(block, sides, width):
    for axis, dim in sides:
        count = lax.axis_size(axis)
        forward = [(i, i + 1) for i in range(count - 1)]
        backward = [(target, source) for source, target in forward]
        low = lax.ppermute(
            lax.slice_in_dim(block, block.shape[dim] - width, None, axis=dim), axis, forward
        )
        high = lax.ppermute(lax.slice_in_dim(block, 0, width, axis=dim), axis, backward)
        block = jnp.concatenate([low, block, high], axis=dim)
    return block


def inverse_rows(spectra):
    row_total = spectra.shape[3]
    row_index = jnp.arange(row_total, dtype=jnp.int32)
    phase_index = row_index[:, None] * row_index[None, :] % row_total
    phase_angle = phase_index.astype(jnp.float32) * (2.0 * jnp.pi / row_total)
    cosine_table = jnp.cos(phase_angle)
    sine_table = jnp.sin(phase_angle)
    real_part = spectra[:, 0]
    imag_part = spectra[:, 1]
    high = lax.Precision.HIGHEST
    out_real = jnp.einsum("yk,mckx->mcxy", cosine_table, real_part, precision=high) - jnp.einsum(
        "yk,mckx->mcxy", sine_table, imag_part, precision=high
    )
    out_imag = jnp.einsum("yk,mckx->mcxy", sine_table, real_part, precision=high) + jnp.einsum(
        "yk,mckx->mcxy", cosine_table, imag_part, precision=high
    )
    scale = 1.0 / jnp.sqrt(jnp.float32(row_total))
    return jnp.stack([out_real, out_imag], axis=1) * scale


def on_device(kspace, kernel, pattern, offsets, segment, temporal_basis):
    frame_total, _, coil_count, row_count, kx_count = kspace.shape
    group_count = kernel.shape[0]
    group_frames = frame_total // group_count
    row_start = lax.axis_index("ky") * row_count
    local_segment = lax.dynamic_slice_in_dim(segment, row_start, row_count)
    acquired = (local_segment[None, :] == pattern[:, None])[:, None, None, :, None]
    zero_fill = jnp.where(acquired, kspace, jnp.zeros_like(kspace))
    padded = padded_2(zero_fill, (("ky", 3),), 1)
    blocks = frame_total // frame_block
    padded_blocks = padded.reshape(blocks, frame_block, 2, coil_count, row_count + 2, kx_count)
    block_group = jnp.arange(blocks, dtype=jnp.int32) * frame_block // group_frames

    def estimate_block(block_item):
        block_data, group_index = block_item
        ky_layers = []
        for ky_tap in range(3):
            ky_slice = block_data[:, :, :, ky_tap : ky_tap + row_count, :]
            ky_layers.append(
                jnp.stack(
                    [
                        jnp.roll(ky_slice, -offsets[kx_tap], axis=4)
                        for kx_tap in range(offsets.shape[0])
                    ],
                    axis=2,
                )
            )
        sources = jnp.stack(ky_layers, axis=2).reshape(frame_block, -1, row_count * kx_count)
        weights = lax.dynamic_index_in_dim(kernel, group_index, 0, keepdims=False)
        return jnp.einsum("io,fir->for", weights, sources, preferred_element_type=jnp.float32)

    estimate = lax.map(estimate_block, (padded_blocks, block_group))
    estimate = estimate.reshape(frame_total, 2, coil_count, row_count, kx_count)
    filled = jnp.where(acquired, kspace.astype(jnp.float32), estimate)
    high = lax.Precision.HIGHEST
    coefficients = jnp.einsum("bf,fpcrx->bpcrx", temporal_basis, filled, precision=high)
    swapped = lax.all_to_all(coefficients, "ky", split_axis=4, concat_axis=3, tiled=True)
    return inverse_rows(swapped)


def solution(mesh):
    return jax.shard_map(
        on_device,
        mesh=mesh,
        in_specs=(P("study", None, None, "ky", None), P(), P("study"), P(), P(), P()),
        out_specs=P("study", None, None, "ky", None),
        check_vma=False,
    )
```

profile of v0, /device:TPU:1, one launch (start us, length us, event | category | flops | bytes accessed | tf_op | source)
XLA Modules:
  0.0 754.4 jit_solution(11994539295915836448)
XLA Ops:
  31.8 13.5 %pad_maximum_fusion.1 = bf16[16,2,32,18,256]{4,3,2,1,0:T(8,128)(2,1)} fusion(bf16[16,2,32,1,256]{4,3,2,1,0:T(2,128)(2,1)S(1)} %copy.40, bf16[16,2,32,16,256]{4,3,2,1,0:T(8,128)(2,1)} %broadcast_select_fusion, bf16[16,2,32,1,256]{4,3,2,1,0:T(2,128)(2,1)S(1)} %copy.39), kind=kLoop, calls=%fused_computation.61 | loop fusion | flops 28311552 | bytes 18874368 | tf_op jit(solution)/shard_map/concatenate | solution.py:18
  45.4 419.9 %while.12 = (s32[]{:T(128)}, f32[4,4,64,4096]{3,2,1,0:T(8,128)}, bf16[4,4,2,32,18,256]{5,4,3,2,1,0:T(8,128)(2,1)}, s32[]{:T(128)}, s32[]{:T(128)}, /*index=5*/s3...) while((s32[]{:T(128)}, f32[4,4,64,4096]{3,2,1,0:T(8,128)}, ...), condition=%wide.region_1.3_spmd, body=%wide.region_0.2_spmd.sunk | while | flops 1723858944 | bytes 229213552 | solution.py:73
  72.6 11.5 %fusion.93 = (bf16[4,2,1,32,16,256]{5,4,3,2,1,0:T(8,128)(2,1)S(1)}, bf16[4,2,1,32,16,256]{5,4,3,2,1,0:T(8,128)(2,1)S(1)}, bf16[4,2,1,32,16,256]{5,4,3,2,1,0:T(8,128)(2,1)S(1)}, bf16[4,2,1,32,16,256]{5,4,3,2,1,0:T(8,128)(2,1)S(1)}) fusion(s32[]{:T(128)S(6)} %select_n.129, bf16[4,2,32,16,256]{4,3,2,1,0:T(8,128)(2,1)} %get-tuple-element.218, ...), kind=kLoop, calls=%fused_computation.34.clone.1 | loop fusion | flops 16777216 | bytes 10485776 | tf_op jit(solution)/shard_map/while/body/eval_jaxpr/stack | solution.py:61
  85.2 10.2 %pad_maximum_fusion.3 = bf16[4,2,3,4,32,16,256]{6,5,4,3,2,1,0:T(8,128)(2,1)} fusion(bf16[4,2,1,4,32,16,256]{6,5,4,3,2,1,0:T(8,128)(2,1)S(1)} %maximum_bitcast_fusion.5, bf16[4,2,1,4,32,16,256]{6,5,4,3,2,1,0:T(8,128)(2,1)S(1)} %get-tuple-element.233, bf16[4,2,1,4,32,16,256]{6,5,4,3,2,1,0:T(8,128)(2,1)S(1)} %get-tuple-element.234), kind=kLoop, calls=%fused_computation.clone.1 | loop fusion | flops 25165824 | bytes 50331648 | tf_op jit(solution)/shard_map/while/body/eval_jaxpr/stack | solution.py:69
  95.4 37.8 %reshape.50 = bf16[4,768,4096]{2,1,0:T(8,128)(2,1)} reshape(bf16[4,2,3,4,32,16,256]{6,5,4,3,2,1,0:T(8,128)(2,1)} %pad_maximum_fusion.3) | data formatting | bytes 50331648 | tf_op jit(solution)/shard_map/while/body/eval_jaxpr/reshape | solution.py:69
  135.8 14.8 %fusion.96 = f32[4,4,64,4096]{3,2,1,0:T(8,128)} fusion(f32[4,4,64,4096]{3,2,1,0:T(8,128)} %get-tuple-element.251, s32[]{:T(128)} %get-tuple-element.250, bf16[4,768,4096]{2,1,0:T(8,128)(2,1)} %reshape.50, bf16[2,768,64]{1,2,0:T(8,128)(2,1)S(1)} %get-tuple-element.273, s32[]{:T(128)S(6)} %select_n.136), kind=kOutput, calls=%fused_computation.29.clone.1 | convolution fusion | flops 1610612736 | bytes 29458948 | tf_op jit(solution)/shard_map/while/body/eval_jaxpr/io,fir->for/dot_general | solution.py:71
  177.5 11.5 %fusion.93 = (bf16[4,2,1,32,16,256]{5,4,3,2,1,0:T(8,128)(2,1)S(1)}, bf16[4,2,1,32,16,256]{5,4,3,2,1,0:T(8,128)(2,1)S(1)}, bf16[4,2,1,32,16,256]{5,4,3,2,1,0:T(8,128)(2,1)S(1)}, bf16[4,2,1,32,16,256]{5,4,3,2,1,0:T(8,128)(2,1)S(1)}) fusion(s32[]{:T(128)S(6)} %select_n.129, bf16[4,2,32,16,256]{4,3,2,1,0:T(8,128)(2,1)} %get-tuple-element.218, ...), kind=kLoop, calls=%fused_computation.34.clone.1 | loop fusion | flops 16777216 | bytes 10485776 | tf_op jit(solution)/shard_map/while/body/eval_jaxpr/stack | solution.py:61
  190.1 10.2 %pad_maximum_fusion.3 = bf16[4,2,3,4,32,16,256]{6,5,4,3,2,1,0:T(8,128)(2,1)} fusion(bf16[4,2,1,4,32,16,256]{6,5,4,3,2,1,0:T(8,128)(2,1)S(1)} %maximum_bitcast_fusion.5, bf16[4,2,1,4,32,16,256]{6,5,4,3,2,1,0:T(8,128)(2,1)S(1)} %get-tuple-element.233, bf16[4,2,1,4,32,16,256]{6,5,4,3,2,1,0:T(8,128)(2,1)S(1)} %get-tuple-element.234), kind=kLoop, calls=%fused_computation.clone.1 | loop fusion | flops 25165824 | bytes 50331648 | tf_op jit(solution)/shard_map/while/body/eval_jaxpr/stack | solution.py:69
  200.3 37.8 %reshape.50 = bf16[4,768,4096]{2,1,0:T(8,128)(2,1)} reshape(bf16[4,2,3,4,32,16,256]{6,5,4,3,2,1,0:T(8,128)(2,1)} %pad_maximum_fusion.3) | data formatting | bytes 50331648 | tf_op jit(solution)/shard_map/while/body/eval_jaxpr/reshape | solution.py:69
  240.7 14.7 %fusion.96 = f32[4,4,64,4096]{3,2,1,0:T(8,128)} fusion(f32[4,4,64,4096]{3,2,1,0:T(8,128)} %get-tuple-element.251, s32[]{:T(128)} %get-tuple-element.250, bf16[4,768,4096]{2,1,0:T(8,128)(2,1)} %reshape.50, bf16[2,768,64]{1,2,0:T(8,128)(2,1)S(1)} %get-tuple-element.273, s32[]{:T(128)S(6)} %select_n.136), kind=kOutput, calls=%fused_computation.29.clone.1 | convolution fusion | flops 1610612736 | bytes 29458948 | tf_op jit(solution)/shard_map/while/body/eval_jaxpr/io,fir->for/dot_general | solution.py:71
  282.3 11.5 %fusion.93 = (bf16[4,2,1,32,16,256]{5,4,3,2,1,0:T(8,128)(2,1)S(1)}, bf16[4,2,1,32,16,256]{5,4,3,2,1,0:T(8,128)(2,1)S(1)}, bf16[4,2,1,32,16,256]{5,4,3,2,1,0:T(8,128)(2,1)S(1)}, bf16[4,2,1,32,16,256]{5,4,3,2,1,0:T(8,128)(2,1)S(1)}) fusion(s32[]{:T(128)S(6)} %select_n.129, bf16[4,2,32,16,256]{4,3,2,1,0:T(8,128)(2,1)} %get-tuple-element.218, ...), kind=kLoop, calls=%fused_computation.34.clone.1 | loop fusion | flops 16777216 | bytes 10485776 | tf_op jit(solution)/shard_map/while/body/eval_jaxpr/stack | solution.py:61
  305.1 37.8 %reshape.50 = bf16[4,768,4096]{2,1,0:T(8,128)(2,1)} reshape(bf16[4,2,3,4,32,16,256]{6,5,4,3,2,1,0:T(8,128)(2,1)} %pad_maximum_fusion.3) | data formatting | bytes 50331648 | tf_op jit(solution)/shard_map/while/body/eval_jaxpr/reshape | solution.py:69
  345.5 14.7 %fusion.96 = f32[4,4,64,4096]{3,2,1,0:T(8,128)} fusion(f32[4,4,64,4096]{3,2,1,0:T(8,128)} %get-tuple-element.251, s32[]{:T(128)} %get-tuple-element.250, bf16[4,768,4096]{2,1,0:T(8,128)(2,1)} %reshape.50, bf16[2,768,64]{1,2,0:T(8,128)(2,1)S(1)} %get-tuple-element.273, s32[]{:T(128)S(6)} %select_n.136), kind=kOutput, calls=%fused_computation.29.clone.1 | convolution fusion | flops 1610612736 | bytes 29458948 | tf_op jit(solution)/shard_map/while/body/eval_jaxpr/io,fir->for/dot_general | solution.py:71
  387.1 11.5 %fusion.93 = (bf16[4,2,1,32,16,256]{5,4,3,2,1,0:T(8,128)(2,1)S(1)}, bf16[4,2,1,32,16,256]{5,4,3,2,1,0:T(8,128)(2,1)S(1)}, bf16[4,2,1,32,16,256]{5,4,3,2,1,0:T(8,128)(2,1)S(1)}, bf16[4,2,1,32,16,256]{5,4,3,2,1,0:T(8,128)(2,1)S(1)}) fusion(s32[]{:T(128)S(6)} %select_n.129, bf16[4,2,32,16,256]{4,3,2,1,0:T(8,128)(2,1)} %get-tuple-element.218, ...), kind=kLoop, calls=%fused_computation.34.clone.1 | loop fusion | flops 16777216 | bytes 10485776 | tf_op jit(solution)/shard_map/while/body/eval_jaxpr/stack | solution.py:61
  409.9 37.8 %reshape.50 = bf16[4,768,4096]{2,1,0:T(8,128)(2,1)} reshape(bf16[4,2,3,4,32,16,256]{6,5,4,3,2,1,0:T(8,128)(2,1)} %pad_maximum_fusion.3) | data formatting | bytes 50331648 | tf_op jit(solution)/shard_map/while/body/eval_jaxpr/reshape | solution.py:69
  450.2 14.7 %fusion.96 = f32[4,4,64,4096]{3,2,1,0:T(8,128)} fusion(f32[4,4,64,4096]{3,2,1,0:T(8,128)} %get-tuple-element.251, s32[]{:T(128)} %get-tuple-element.250, bf16[4,768,4096]{2,1,0:T(8,128)(2,1)} %reshape.50, bf16[2,768,64]{1,2,0:T(8,128)(2,1)S(1)} %get-tuple-element.273, s32[]{:T(128)S(6)} %select_n.136), kind=kOutput, calls=%fused_computation.29.clone.1 | convolution fusion | flops 1610612736 | bytes 29458948 | tf_op jit(solution)/shard_map/while/body/eval_jaxpr/io,fir->for/dot_general | solution.py:71
  465.3 11.0 %copy.54 = f32[128,8,16,256]{3,2,1,0:T(8,128)S(1)} copy(f32[128,8,16,256]{3,1,2,0:T(8,128)} %bitcast.126) | data formatting | bytes 33554432
  482.5 17.8 %fusion.30 = f32[5,2,32,16,256]{4,0,3,2,1:T(8,128)} fusion(f32[16,2,32,16,256]{4,3,2,1,0:T(8,128)S(1)} %convert_select_fusion, f32[5,16]{1,0:T(8,128)S(1)} %copy-done), kind=kOutput, calls=%fused_computation.64 | convolution fusion | flops 251658240 | bytes 22020416 | tf_op jit(solution)/shard_map/bf,fpcrx->bpcrx/dot_general | solution.py:77
  500.3 14.0 %copy.42 = f32[5,2,32,16,256]{2,3,1,0,4:T(8,128)} copy(f32[5,2,32,16,256]{4,0,3,2,1:T(8,128)} %fusion.30) | data formatting | bytes 10485760 | tf_op jit(solution)/shard_map/bf,fpcrx->bpcrx/dot_general | solution.py:77
  514.2 18.0 %reshape.47 = f32[16,1,81920]{2,1,0:T(1,128)} reshape(f32[256,5,2,16,32]{4,3,2,1,0:T(8,128)} %bitcast.122) | data formatting | bytes 10485760
  532.2 121.4 %all_to_all.18 = f32[16,1,81920]{2,1,0:T(1,128)} all-to-all(f32[16,1,81920]{2,1,0:T(1,128)} %reshape.47), channel_id=1, replica_groups=mesh['study'=2,'ky'=16] {'ky'}, dimensions={0} | all-to-all | bytes 10485760 | tf_op jit(solution)/shard_map/all_to_all | solution.py:78
  654.2 16.9 %reduce = f32[16,81920]{1,0:T(8,128)} reduce(f32[16,1,81920]{2,1,0:T(1,128)} %all_to_all.18, f32[]{:T(128)} %broadcast.61), dimensions={1}, to_apply=%all_to_all.13.reduce_sub_computation | reduce | bytes 10485764 | tf_op jit(solution)/shard_map/all_to_all | solution.py:78
  671.1 18.1 %reshape.48 = f32[256,5,2,16,32]{4,3,2,1,0:T(8,128)} reshape(f32[16,81920]{1,0:T(8,128)} %reduce) | data formatting | bytes 10485760
  689.2 18.5 %copy.44 = f32[5,2,32,16,16,16]{2,5,4,3,1,0:T(8,128)S(1)} copy(f32[5,2,32,16,16,16]{2,4,1,0,5,3:T(8,128)} %bitcast.123) | data formatting | bytes 10485760 | tf_op jit(solution)/shard_map/all_to_all | solution.py:78
  (68 shorter events, 217.1 us)
Async XLA Ops:
  0.0 482.5 %copy-start = (f32[5,16]{1,0:T(8,128)S(1)}, f32[5,16]{1,0:T(8,128)}, u32[]{:S(2)}) copy-start(f32[5,16]{1,0:T(8,128)} %param.15) | copy-start | bytes 964
  1.5 7.2 copy-start.3
  8.7 11.3 %copy-start.5 = (s32[4]{0:T(128)S(1)}, s32[4]{0:T(128)}, u32[]{:S(2)}) copy-start(s32[4]{0:T(128)} %param.13) | copy-start | bytes 52
  13.5 16.3 %collective-permute-start = (bf16[16,2,32,1,256]{4,2,3,1,0:T(8,128)(2,1)S(1)}, bf16[16,2,32,1,256]{4,2,3,1,0:T(8,128)(2,1)S(1)}, u32[]{:S(2)}, u32[]{:S(2)}) collective-permute-start(bf16[16,2,32,1,256]{4,2,3,1,0:T(8,128)(2,1)S(1)} %copy.37), channel_id=1, source_target_pairs={{0,1},{1,2},{2,3},{3,4},{4,5},{5,6},{6,7},{7,8},{8,9},{9,10},{10,1... | collective-permute-start | bytes 1572872 | tf_op jit(solution)/shard_map/ppermute | solution.py:14
  18.1 12.6 %collective-permute-start.1 = (bf16[16,2,32,1,256]{4,2,3,1,0:T(8,128)(2,1)S(1)}, bf16[16,2,32,1,256]{4,2,3,1,0:T(8,128)(2,1)S(1)}, u32[]{:S(2)}, u32[]{:S(2)}) collective-permute-start(bf16[16,2,32,1,256]{4,2,3,1,0:T(8,128)(2,1)S(1)} %copy.38), channel_id=1, source_target_pairs={{1,0},{2,1},{3,2},{4,3},{5,4},{6,5},{7,6},{8,7},{9,8},{10,9},{11,1... | collective-permute-start | bytes 1572872 | tf_op jit(solution)/shard_map/ppermute | solution.py:17
  31.8 13.6 %copy-start.2 = (bf16[2,768,64]{1,2,0:T(8,128)(2,1)S(1)}, bf16[2,768,64]{1,2,0:T(8,128)(2,1)}, u32[]{:S(2)}) copy-start(bf16[2,768,64]{1,2,0:T(8,128)(2,1)} %param.11) | copy-start | bytes 589828
  465.3 11.0 %copy-start.4 = (pred[16,16]{1,0:T(8,128)(4,1)S(1)}, pred[16,16]{1,0:T(8,128)(4,1)}, u32[]{:S(2)}) copy-start(pred[16,16]{1,0:T(8,128)(4,1)} %copy-done.3) | copy-start | bytes 772
  742.0 5.1 copy-start.1
where the time goes:
time: 765 us; the launch traced here: 754 us
  local copies, waits for them, and re-layouts  289 us (38%)
  other arithmetic  225 us (29%)
  blocking collectives  121 us (16%)
  matrix products  94.5 us (12%)
  loops' own time  8.59 us (1%)
    reshape x4, local copies, waits for them, and re-layouts, estimate_block(): jnp.stack(ky_layers, axis=2).reshape(frame_block, -1, row_count * kx_count)  151 us
    all_to_all x1, blocking collectives, on_device(): lax.all_to_all(coefficients, 'ky', split_axis=4, concat_axis=3, tiled=True)  121 us
    another operation x12, other arithmetic, estimate_block(): jnp.stack([jnp.roll(ky_slice, -offsets[kx_tap], axis=4) for kx_tap in ran...  111 us
    another operation x12, other arithmetic, estimate_block(): jnp.stack(ky_layers, axis=2).reshape(frame_block, -1, row_count * kx_count)  68.6 us
    unnamed x17, local copies, waits for them, and re-layouts  64.4 us
    dot_general x4, matrix products, estimate_block(): jnp.einsum('io,fir->for', weights, sources, preferred_element_type=jnp.fl...  58.8 us
    all_to_all x2, local copies, waits for them, and re-layouts, on_device(): lax.all_to_all(coefficients, 'ky', split_axis=4, concat_axis=3, tiled=True)  19 us
    dot_general x1, matrix products, on_device(): jnp.einsum('bf,fpcrx->bpcrx', temporal_basis, filled, precision=high)  17.8 us
  transfers between devices with their start and end apart: 2, of which 1 were waited for; matrix products, arithmetic and copies ran while one was open for 0% of the time, Pallas kernels for 0%

commit v1 on v0

--- a/solution.py
+++ b/solution.py
@@ -75,7 +75,18 @@
     filled = jnp.where(acquired, kspace.astype(jnp.float32), estimate)
     high = lax.Precision.HIGHEST
     coefficients = jnp.einsum("bf,fpcrx->bpcrx", temporal_basis, filled, precision=high)
-    swapped = lax.all_to_all(coefficients, "ky", split_axis=4, concat_axis=3, tiled=True)
+    ways, here = (lax.axis_size("ky"), lax.axis_index("ky"))
+    width_2 = coefficients.shape[4] // ways
+    shape = list(coefficients.shape)
+    shape[4] = width_2
+    height = shape[3]
+    shape[3] = height * ways
+    swapped = jnp.zeros(shape, coefficients.dtype)
+    for mask in range(ways):
+        part = lax.dynamic_slice_in_dim(coefficients, (here ^ mask) * width_2, width_2, axis=4)
+        if mask:
+            part = lax.ppermute(part, "ky", [(d, d ^ mask) for d in range(ways)])
+        swapped = lax.dynamic_update_slice_in_dim(swapped, part, (here ^ mask) * height, axis=3)
     return inverse_rows(swapped)
 
 

time: 765 us -> 1750 us (2.29)
  local copies, waits for them, and re-layouts: 289 us -> 1090 us
  waiting for transfers between devices: 6.45 us -> 290 us
  blocking collectives: 121 us -> 0 us
  starting transfers between devices: 6.45 us -> 29.3 us
    dynamic_update_slice x0 -> x16, local copies, waits for them, and re-layouts: none -> 770 us  [on_device(): lax.dynamic_update_slice_in_dim(swapped, part, (here ^ mask) * height, ax...]
    ppermute x0 -> x15, waiting for transfers between devices: none -> 284 us  [on_device(): part = lax.ppermute(part, 'ky', [(d, d ^ mask) for d in range(ways)])]
    all_to_all x1 -> x0, blocking collectives: 121 us -> none  [on_device(): lax.all_to_all(coefficients, 'ky', split_axis=4, concat_axis=3, tiled=True)]
    dynamic_slice x0 -> x17, local copies, waits for them, and re-layouts: none -> 83.6 us  [on_device(): lax.dynamic_slice_in_dim(coefficients, (here ^ mask) * width_2, width_2,...]
    unnamed x17 -> x21, local copies, waits for them, and re-layouts: 64.4 us -> 11.5 us
    ppermute x0 -> x15, local copies, waits for them, and re-layouts: none -> 37.3 us  [on_device(): part = lax.ppermute(part, 'ky', [(d, d ^ mask) for d in range(ways)])]
    ppermute x0 -> x15, starting transfers between devices: none -> 22.8 us  [on_device(): part = lax.ppermute(part, 'ky', [(d, d ^ mask) for d in range(ways)])]
    all_to_all x2 -> x0, local copies, waits for them, and re-layouts: 19 us -> none  [on_device(): lax.all_to_all(coefficients, 'ky', split_axis=4, concat_axis=3, tiled=True)]
  transfers between devices with their start and end apart: 2 -> 17, of which waited for: 1 -> 7; matrix products, arithmetic and copies ran while one was open for 0% -> 47% of each run, Pallas kernels for 0% -> 0%
where the time goes in v1:
time: 1750 us; the launch traced here: 1740 us
  local copies, waits for them, and re-layouts  1090 us (62%)
  waiting for transfers between devices  290 us (17%)
  other arithmetic  209 us (12%)
  matrix products  96.6 us (6%)
  starting transfers between devices  29.3 us (2%)
  loops' own time  20.4 us (1%)
    dynamic_update_slice x16, local copies, waits for them, and re-layouts, on_device(): lax.dynamic_update_slice_in_dim(swapped, part, (here ^ mask) * height, ax...  770 us
    ppermute x15, waiting for transfers between devices, on_device(): part = lax.ppermute(part, 'ky', [(d, d ^ mask) for d in range(ways)])  284 us
    reshape x4, local copies, waits for them, and re-layouts, estimate_block(): jnp.stack(ky_layers, axis=2).reshape(frame_block, -1, row_count * kx_count)  151 us
    another operation x12, other arithmetic, estimate_block(): jnp.stack([jnp.roll(ky_slice, -offsets[kx_tap], axis=4) for kx_tap in ran...  111 us
    dynamic_slice x17, local copies, waits for them, and re-layouts, on_device(): lax.dynamic_slice_in_dim(coefficients, (here ^ mask) * width_2, width_2,...  83.6 us
    another operation x12, other arithmetic, estimate_block(): jnp.stack(ky_layers, axis=2).reshape(frame_block, -1, row_count * kx_count)  68.8 us
    dot_general x4, matrix products, estimate_block(): jnp.einsum('io,fir->for', weights, sources, preferred_element_type=jnp.fl...  58.9 us
    ppermute x15, local copies, waits for them, and re-layouts, on_device(): part = lax.ppermute(part, 'ky', [(d, d ^ mask) for d in range(ways)])  37.3 us
  transfers between devices with their start and end apart: 17, of which 7 were waited for; matrix products, arithmetic and copies ran while one was open for 47% of the time, Pallas kernels for 0%

profile of v1, /device:TPU:1, one launch (start us, length us, event | category | flops | bytes accessed | tf_op | source)
XLA Modules:
  0.0 1739.1 jit_solution(924499190047031925)
XLA Ops:
  45.4 432.2 %while.12 = (s32[]{:T(128)}, f32[4,4,64,4096]{3,2,1,0:T(8,128)}, bf16[4,4,2,32,18,256]{5,4,3,2,1,0:T(8,128)(2,1)}, s32[]{:T(128)}, s32[]{:T(128)}, /*index=5*/s3...) while((s32[]{:T(128)}, f32[4,4,64,4096]{3,2,1,0:T(8,128)}, ...), condition=%wide.region_1.3_spmd, body=%wide.region_0.2_spmd.sunk | while | flops 1723858944 | bytes 229213552 | solution.py:73
  107.3 37.8 %reshape.48 = bf16[4,768,4096]{2,1,0:T(8,128)(2,1)} reshape(bf16[4,2,3,4,32,16,256]{6,5,4,3,2,1,0:T(8,128)(2,1)} %pad_maximum_fusion.3) | data formatting | bytes 50331648 | tf_op jit(solution)/shard_map/while/body/eval_jaxpr/reshape | solution.py:69
  212.3 37.8 %reshape.48 = bf16[4,768,4096]{2,1,0:T(8,128)(2,1)} reshape(bf16[4,2,3,4,32,16,256]{6,5,4,3,2,1,0:T(8,128)(2,1)} %pad_maximum_fusion.3) | data formatting | bytes 50331648 | tf_op jit(solution)/shard_map/while/body/eval_jaxpr/reshape | solution.py:69
  317.2 37.8 %reshape.48 = bf16[4,768,4096]{2,1,0:T(8,128)(2,1)} reshape(bf16[4,2,3,4,32,16,256]{6,5,4,3,2,1,0:T(8,128)(2,1)} %pad_maximum_fusion.3) | data formatting | bytes 50331648 | tf_op jit(solution)/shard_map/while/body/eval_jaxpr/reshape | solution.py:69
  422.1 37.8 %reshape.48 = bf16[4,768,4096]{2,1,0:T(8,128)(2,1)} reshape(bf16[4,2,3,4,32,16,256]{6,5,4,3,2,1,0:T(8,128)(2,1)} %pad_maximum_fusion.3) | data formatting | bytes 50331648 | tf_op jit(solution)/shard_map/while/body/eval_jaxpr/reshape | solution.py:69
  496.0 22.4 %fusion.28 = f32[2,32,16,256,5]{3,4,2,1,0:T(8,128)S(1)} fusion(f32[16,2,32,16,256]{4,3,2,1,0:T(8,128)} %convert_select_fusion, f32[5,16]{1,0:T(8,128)S(1)} %copy-done), kind=kOutput, calls=%fused_computation.58 | convolution fusion | flops 251658240 | bytes 22020416 | tf_op jit(solution)/shard_map/bf,fpcrx->bpcrx/dot_general | solution.py:77
  518.4 25.0 %dynamic-slice_bitcast_fusion.1 = (f32[5,2,32,16,16]{4,0,3,2,1:T(8,128)}, f32[5,2,32,16,16]{4,0,3,2,1:T(8,128)}, f32[5,2,32,16,16]{4,0,3,2,1:T(8,128)}, f32[5,2,...) fusion(f32[2,32,16,256,5]{3,4,2,1,0:T(8,128)S(1)} %fusion.28, ...), kind=kLoop, calls=%fused_computation.64 | loop fusion | bytes 10485824 | tf_op jit(solution)/shard_map/dynamic_slice | solution.py:86
  617.6 59.1 %collective-permute-done.6 = f32[5,2,32,16,16]{2,4,3,1,0:T(8,128)} collective-permute-done((f32[5,2,32,16,16]{2,4,3,1,0:T(8,128)}, f32[5,2,32,16,16]{2,4,3,1,0:T(8,128)}, u32[]{:S(2)}, u32[]{:S(2)}) %collective-permute-start.6) | collective-permute-done | bytes 327712 | tf_op jit(solution)/shard_map/ppermute | solution.py:88
  706.5 27.2 %collective-permute-done.8 = f32[5,2,32,16,16]{2,4,3,1,0:T(8,128)} collective-permute-done((f32[5,2,32,16,16]{2,4,3,1,0:T(8,128)}, f32[5,2,32,16,16]{2,4,3,1,0:T(8,128)}, u32[]{:S(2)}, u32[]{:S(2)}) %collective-permute-start.8) | collective-permute-done | bytes 327712 | tf_op jit(solution)/shard_map/ppermute | solution.py:88
  747.7 156.4 %collective-permute-done.11 = f32[5,2,32,16,16]{2,4,3,1,0:T(8,128)S(1)} collective-permute-done((f32[5,2,32,16,16]{2,4,3,1,0:T(8,128)}, f32[5,2,32,16,16]{2,4,3,1,0:T(8,128)S(1)}, u32[]{:S(2)}, u32[]{:S(2)}) %collective-permute-start.11) | collective-permute-done | bytes 327712 | tf_op jit(solution)/shard_map/ppermute | solution.py:88
  911.7 53.3 %dynamic_update_slice.54 = f32[5,2,32,256,16]{3,4,2,0,1:T(8,128)} dynamic-update-slice(f32[5,2,32,256,16]{3,4,2,0,1:T(8,128)} %broadcast_in_dim.34, f32[5,2,32,16,16]{3,4,2,0,1:T(8,128)S(1)} %copy.66, s32[]{:T(128)} %constant.91.clone.1, s32[]{:T(128)} %constant.91.clone.1, s32[]{:T(128)} %constant.91.clone.1, s32[]{:T(128)S(6)} %select_n.106, s32[]{:T(128)} %constant.91.clone.1) | dynamic-update-slice | bytes 655364 | tf_op jit(solution)/shard_map/dynamic_update_slice | solution.py:89
  984.9 53.3 %dynamic_update_slice.56 = f32[5,2,32,256,16]{3,4,2,0,1:T(8,128)} dynamic-update-slice(f32[5,2,32,256,16]{3,4,2,0,1:T(8,128)} %dynamic_update_slice.55, f32[5,2,32,16,16]{3,4,2,0,1:T(8,128)S(1)} %copy.70, s32[]{:T(128)} %constant.91.clone.1, s32[]{:T(128)} %constant.91.clone.1, s32[]{:T(128)} %constant.91.clone.1, s32[]{:T(128)S(6)} %select_n.111, s32[]{:T(128)} %constant.91.clone.1) | dynamic-update-slice | bytes 655364 | tf_op jit(solution)/shard_map/dynamic_update_slice | solution.py:89
  1040.7 53.3 %dynamic_update_slice.57 = f32[5,2,32,256,16]{3,4,2,0,1:T(8,128)} dynamic-update-slice(f32[5,2,32,256,16]{3,4,2,0,1:T(8,128)} %dynamic_update_slice.56, f32[5,2,32,16,16]{3,4,2,0,1:T(8,128)S(1)} %copy.72, s32[]{:T(128)} %constant.91.clone.1, s32[]{:T(128)} %constant.91.clone.1, s32[]{:T(128)} %constant.91.clone.1, s32[]{:T(128)S(6)} %select_n.112, s32[]{:T(128)} %constant.91.clone.1) | dynamic-update-slice | bytes 655364 | tf_op jit(solution)/shard_map/dynamic_update_slice | solution.py:89
  1096.5 53.3 %dynamic_update_slice.58 = f32[5,2,32,256,16]{3,4,2,0,1:T(8,128)} dynamic-update-slice(f32[5,2,32,256,16]{3,4,2,0,1:T(8,128)} %dynamic_update_slice.57, f32[5,2,32,16,16]{3,4,2,0,1:T(8,128)S(1)} %copy.74, s32[]{:T(128)} %constant.91.clone.1, s32[]{:T(128)} %constant.91.clone.1, s32[]{:T(128)} %constant.91.clone.1, s32[]{:T(128)S(6)} %select_n.113, s32[]{:T(128)} %constant.91.clone.1) | dynamic-update-slice | bytes 655364 | tf_op jit(solution)/shard_map/dynamic_update_slice | solution.py:89
  1152.3 53.3 %dynamic_update_slice.59 = f32[5,2,32,256,16]{3,4,2,0,1:T(8,128)} dynamic-update-slice(f32[5,2,32,256,16]{3,4,2,0,1:T(8,128)} %dynamic_update_slice.58, f32[5,2,32,16,16]{3,4,2,0,1:T(8,128)S(1)} %copy.76, s32[]{:T(128)} %constant.91.clone.1, s32[]{:T(128)} %constant.91.clone.1, s32[]{:T(128)} %constant.91.clone.1, s32[]{:T(128)S(6)} %select_n.114, s32[]{:T(128)} %constant.91.clone.1) | dynamic-update-slice | bytes 655364 | tf_op jit(solution)/shard_map/dynamic_update_slice | solution.py:89
  1208.1 53.3 %dynamic_update_slice.60 = f32[5,2,32,256,16]{3,4,2,0,1:T(8,128)} dynamic-update-slice(f32[5,2,32,256,16]{3,4,2,0,1:T(8,128)} %dynamic_update_slice.59, f32[5,2,32,16,16]{3,4,2,0,1:T(8,128)S(1)} %copy.78, s32[]{:T(128)} %constant.91.clone.1, s32[]{:T(128)} %constant.91.clone.1, s32[]{:T(128)} %constant.91.clone.1, s32[]{:T(128)S(6)} %select_n.115, s32[]{:T(128)} %constant.91.clone.1) | dynamic-update-slice | bytes 655364 | tf_op jit(solution)/shard_map/dynamic_update_slice | solution.py:89
  1263.9 53.3 %dynamic_update_slice.61 = f32[5,2,32,256,16]{3,4,2,0,1:T(8,128)} dynamic-update-slice(f32[5,2,32,256,16]{3,4,2,0,1:T(8,128)} %dynamic_update_slice.60, f32[5,2,32,16,16]{3,4,2,0,1:T(8,128)S(1)} %copy.80, s32[]{:T(128)} %constant.91.clone.1, s32[]{:T(128)} %constant.91.clone.1, s32[]{:T(128)} %constant.91.clone.1, s32[]{:T(128)S(6)} %select_n.116, s32[]{:T(128)} %constant.91.clone.1) | dynamic-update-slice | bytes 655364 | tf_op jit(solution)/shard_map/dynamic_update_slice | solution.py:89
  1319.7 52.7 %dynamic_update_slice.62 = f32[5,2,32,256,16]{3,4,2,0,1:T(8,128)} dynamic-update-slice(f32[5,2,32,256,16]{3,4,2,0,1:T(8,128)} %dynamic_update_slice.61, f32[5,2,32,16,16]{3,4,2,0,1:T(8,128)S(1)} %copy.82, s32[]{:T(128)} %constant.91.clone.1, s32[]{:T(128)} %constant.91.clone.1, s32[]{:T(128)} %constant.91.clone.1, s32[]{:T(128)S(6)} %select_n.117, s32[]{:T(128)} %constant.91.clone.1) | dynamic-update-slice | bytes 655364 | tf_op jit(solution)/shard_map/dynamic_update_slice | solution.py:89
  1391.1 52.7 %dynamic_update_slice.64 = f32[5,2,32,256,16]{3,4,2,0,1:T(8,128)} dynamic-update-slice(f32[5,2,32,256,16]{3,4,2,0,1:T(8,128)} %dynamic_update_slice.63, f32[5,2,32,16,16]{3,4,2,0,1:T(8,128)S(1)} %copy.86, s32[]{:T(128)} %constant.91.clone.1, s32[]{:T(128)} %constant.91.clone.1, s32[]{:T(128)} %constant.91.clone.1, s32[]{:T(128)S(6)} %select_n.119, s32[]{:T(128)} %constant.91.clone.1) | dynamic-update-slice | bytes 655364 | tf_op jit(solution)/shard_map/dynamic_update_slice | solution.py:89
  1446.3 52.7 %dynamic_update_slice.65 = f32[5,2,32,256,16]{3,4,2,0,1:T(8,128)} dynamic-update-slice(f32[5,2,32,256,16]{3,4,2,0,1:T(8,128)} %dynamic_update_slice.64, f32[5,2,32,16,16]{3,4,2,0,1:T(8,128)S(1)} %copy.88, s32[]{:T(128)} %constant.91.clone.1, s32[]{:T(128)} %constant.91.clone.1, s32[]{:T(128)} %constant.91.clone.1, s32[]{:T(128)S(6)} %select_n.120, s32[]{:T(128)} %constant.91.clone.1) | dynamic-update-slice | bytes 655364 | tf_op jit(solution)/shard_map/dynamic_update_slice | solution.py:89
  1501.5 52.7 %dynamic_update_slice.66 = f32[5,2,32,256,16]{3,4,2,0,1:T(8,128)} dynamic-update-slice(f32[5,2,32,256,16]{3,4,2,0,1:T(8,128)} %dynamic_update_slice.65, f32[5,2,32,16,16]{3,4,2,0,1:T(8,128)S(1)} %copy.90, s32[]{:T(128)} %constant.91.clone.1, s32[]{:T(128)} %constant.91.clone.1, s32[]{:T(128)} %constant.91.clone.1, s32[]{:T(128)S(6)} %select_n.121, s32[]{:T(128)} %constant.91.clone.1) | dynamic-update-slice | bytes 655364 | tf_op jit(solution)/shard_map/dynamic_update_slice | solution.py:89
  1556.6 52.7 %dynamic_update_slice.67 = f32[5,2,32,256,16]{3,4,2,0,1:T(8,128)} dynamic-update-slice(f32[5,2,32,256,16]{3,4,2,0,1:T(8,128)} %dynamic_update_slice.66, f32[5,2,32,16,16]{3,4,2,0,1:T(8,128)S(1)} %copy.92, s32[]{:T(128)} %constant.91.clone.1, s32[]{:T(128)} %constant.91.clone.1, s32[]{:T(128)} %constant.91.clone.1, s32[]{:T(128)S(6)} %select_n.122, s32[]{:T(128)} %constant.91.clone.1) | dynamic-update-slice | bytes 655364 | tf_op jit(solution)/shard_map/dynamic_update_slice | solution.py:89
  1611.8 52.7 %dynamic_update_slice.68 = f32[5,2,32,256,16]{3,4,2,0,1:T(8,128)} dynamic-update-slice(f32[5,2,32,256,16]{3,4,2,0,1:T(8,128)} %dynamic_update_slice.67, f32[5,2,32,16,16]{3,4,2,0,1:T(8,128)S(1)} %copy.94, s32[]{:T(128)} %constant.91.clone.1, s32[]{:T(128)} %constant.91.clone.1, s32[]{:T(128)} %constant.91.clone.1, s32[]{:T(128)S(6)} %select_n.123, s32[]{:T(128)} %constant.91.clone.1) | dynamic-update-slice | bytes 655364 | tf_op jit(solution)/shard_map/dynamic_update_slice | solution.py:89
  1666.9 52.8 %dynamic_update_slice.69 = f32[5,2,32,256,16]{3,4,2,0,1:T(8,128)} dynamic-update-slice(f32[5,2,32,256,16]{3,4,2,0,1:T(8,128)} %dynamic_update_slice.68, f32[5,2,32,16,16]{3,4,2,0,1:T(8,128)S(1)} %copy.96, s32[]{:T(128)} %constant.91.clone.1, s32[]{:T(128)} %constant.91.clone.1, s32[]{:T(128)} %constant.91.clone.1, s32[]{:T(128)S(6)} %select_n.124, s32[]{:T(128)} %constant.91.clone.1) | dynamic-update-slice | bytes 655364 | tf_op jit(solution)/shard_map/dynamic_update_slice | solution.py:89
  (145 shorter events, 531.6 us)
Async XLA Ops:
  0.0 496.0 %copy-start = (f32[5,16]{1,0:T(8,128)S(1)}, f32[5,16]{1,0:T(8,128)}, u32[]{:S(2)}) copy-start(f32[5,16]{1,0:T(8,128)} %param.15) | copy-start | bytes 964
  8.8 11.4 copy-start.9
  13.5 16.3 collective-permute-start
  18.2 12.6 collective-permute-start.1
  31.9 13.5 copy-start.6
  477.6 11.4 copy-start.2
  477.6 11.4 copy-start.8
  547.2 30.2 %collective-permute-start.2 = (f32[5,2,32,16,16]{2,4,3,1,0:T(8,128)}, f32[5,2,32,16,16]{2,4,3,1,0:T(8,128)S(1)}, u32[]{:S(2)}, u32[]{:S(2)}) collective-permute-start(f32[5,2,32,16,16]{2,4,3,1,0:T(8,128)} %copy.67), channel_id=1, source_target_pairs={{0,1},{1,0},{2,3},{3,2},{4,5},{5,4},{6,7},{7,6},{8,9},{9,8},{10,11... | collective-permute-start | bytes 983048 | tf_op jit(solution)/shard_map/ppermute | solution.py:88
  550.9 32.1 %collective-permute-start.3 = (f32[5,2,32,16,16]{2,4,3,1,0:T(8,128)}, f32[5,2,32,16,16]{2,4,3,1,0:T(8,128)S(1)}, u32[]{:S(2)}, u32[]{:S(2)}) collective-permute-start(f32[5,2,32,16,16]{2,4,3,1,0:T(8,128)} %copy.69), channel_id=1, source_target_pairs={{0,2},{1,3},{2,0},{3,1},{4,6},{5,7},{6,4},{7,5},{8,10},{9,11},{10,... | collective-permute-start | bytes 983048 | tf_op jit(solution)/shard_map/ppermute | solution.py:88
  557.1 54.1 %collective-permute-start.4 = (f32[5,2,32,16,16]{2,4,3,1,0:T(8,128)}, f32[5,2,32,16,16]{2,4,3,1,0:T(8,128)}, u32[]{:S(2)}, u32[]{:S(2)}) collective-permute-start(f32[5,2,32,16,16]{2,4,3,1,0:T(8,128)} %copy.71), channel_id=1, source_target_pairs={{0,3},{1,2},{2,1},{3,0},{4,7},{5,6},{6,5},{7,4},{8,11},{9,10},{10,... | collective-permute-start | bytes 983048 | tf_op jit(solution)/shard_map/ppermute | solution.py:88
  560.8 52.7 %collective-permute-start.5 = (f32[5,2,32,16,16]{2,4,3,1,0:T(8,128)}, f32[5,2,32,16,16]{2,4,3,1,0:T(8,128)}, u32[]{:S(2)}, u32[]{:S(2)}) collective-permute-start(f32[5,2,32,16,16]{2,4,3,1,0:T(8,128)} %copy.73), channel_id=1, source_target_pairs={{0,4},{1,5},{2,6},{3,7},{4,0},{5,1},{6,2},{7,3},{8,12},{9,13},{10,... | collective-permute-start | bytes 983048 | tf_op jit(solution)/shard_map/ppermute | solution.py:88
  565.8 110.9 %collective-permute-start.6 = (f32[5,2,32,16,16]{2,4,3,1,0:T(8,128)}, f32[5,2,32,16,16]{2,4,3,1,0:T(8,128)}, u32[]{:S(2)}, u32[]{:S(2)}) collective-permute-start(f32[5,2,32,16,16]{2,4,3,1,0:T(8,128)} %copy.75), channel_id=1, source_target_pairs={{0,5},{1,4},{2,7},{3,6},{4,1},{5,0},{6,3},{7,2},{8,13},{9,12},{10,... | collective-permute-start | bytes 983048 | tf_op jit(solution)/shard_map/ppermute | solution.py:88
  577.5 40.2 %copy-start.3 = (f32[5,2,32,16,16]{2,4,3,1,0:T(8,128)}, f32[5,2,32,16,16]{2,4,3,1,0:T(8,128)S(1)}, u32[]{:S(2)}) copy-start(f32[5,2,32,16,16]{2,4,3,1,0:T(8,128)S(1)} %collective-permute-done.2) | copy-start | bytes 983044
  577.5 127.6 %collective-permute-start.7 = (f32[5,2,32,16,16]{2,4,3,1,0:T(8,128)}, f32[5,2,32,16,16]{2,4,3,1,0:T(8,128)}, u32[]{:S(2)}, u32[]{:S(2)}) collective-permute-start(f32[5,2,32,16,16]{2,4,3,1,0:T(8,128)} %copy.77), channel_id=1, source_target_pairs={{0,6},{1,7},{2,4},{3,5},{4,2},{5,3},{6,0},{7,1},{8,14},{9,15},{10,... | collective-permute-start | bytes 983048 | tf_op jit(solution)/shard_map/ppermute | solution.py:88
  582.9 34.7 %copy-start.4 = (f32[5,2,32,16,16]{2,4,3,1,0:T(8,128)}, f32[5,2,32,16,16]{2,4,3,1,0:T(8,128)S(1)}, u32[]{:S(2)}) copy-start(f32[5,2,32,16,16]{2,4,3,1,0:T(8,128)S(1)} %collective-permute-done.3) | copy-start | bytes 983044
  582.9 150.8 %collective-permute-start.8 = (f32[5,2,32,16,16]{2,4,3,1,0:T(8,128)}, f32[5,2,32,16,16]{2,4,3,1,0:T(8,128)}, u32[]{:S(2)}, u32[]{:S(2)}) collective-permute-start(f32[5,2,32,16,16]{2,4,3,1,0:T(8,128)} %copy.79), channel_id=1, source_target_pairs={{0,7},{1,6},{2,5},{3,4},{4,3},{5,2},{6,1},{7,0},{8,15},{9,14},{10,... | collective-permute-start | bytes 983048 | tf_op jit(solution)/shard_map/ppermute | solution.py:88
  611.2 128.2 %collective-permute-start.9 = (f32[5,2,32,16,16]{2,4,3,1,0:T(8,128)}, f32[5,2,32,16,16]{2,4,3,1,0:T(8,128)}, u32[]{:S(2)}, u32[]{:S(2)}) collective-permute-start(f32[5,2,32,16,16]{2,4,3,1,0:T(8,128)} %copy.81), channel_id=1, source_target_pairs={{0,8},{1,9},{2,10},{3,11},{4,12},{5,13},{6,14},{7,15},{8,0},{9,1},... | collective-permute-start | bytes 983048 | tf_op jit(solution)/shard_map/ppermute | solution.py:88
  613.5 127.1 %collective-permute-start.10 = (f32[5,2,32,16,16]{2,4,3,1,0:T(8,128)}, f32[5,2,32,16,16]{2,4,3,1,0:T(8,128)}, u32[]{:S(2)}, u32[]{:S(2)}) collective-permute-start(f32[5,2,32,16,16]{2,4,3,1,0:T(8,128)} %copy.83), channel_id=1, source_target_pairs={{0,9},{1,8},{2,11},{3,10},{4,13},{5,12},{6,15},{7,14},{8,1},{9,0},... | collective-permute-start | bytes 983048 | tf_op jit(solution)/shard_map/ppermute | solution.py:88
  676.7 227.4 %collective-permute-start.11 = (f32[5,2,32,16,16]{2,4,3,1,0:T(8,128)}, f32[5,2,32,16,16]{2,4,3,1,0:T(8,128)S(1)}, u32[]{:S(2)}, u32[]{:S(2)}) collective-permute-start(f32[5,2,32,16,16]{2,4,3,1,0:T(8,128)} %copy.85), channel_id=1, source_target_pairs={{0,10},{1,11},{2,8},{3,9},{4,14},{5,15},{6,12},{7,13},{8,2},{9,3},... | collective-permute-start | bytes 983048 | tf_op jit(solution)/shard_map/ppermute | solution.py:88
  705.0 738.8 %collective-permute-start.12 = (f32[5,2,32,16,16]{2,4,3,1,0:T(8,128)}, f32[5,2,32,16,16]{2,4,3,1,0:T(8,128)}, u32[]{:S(2)}, u32[]{:S(2)}) collective-permute-start(f32[5,2,32,16,16]{2,4,3,1,0:T(8,128)} %copy.87), channel_id=1, source_target_pairs={{0,11},{1,10},{2,9},{3,8},{4,15},{5,14},{6,13},{7,12},{8,3},{9,2},... | collective-permute-start | bytes 983048 | tf_op jit(solution)/shard_map/ppermute | solution.py:88
  733.7 765.3 %collective-permute-start.13 = (f32[5,2,32,16,16]{2,4,3,1,0:T(8,128)}, f32[5,2,32,16,16]{2,4,3,1,0:T(8,128)}, u32[]{:S(2)}, u32[]{:S(2)}) collective-permute-start(f32[5,2,32,16,16]{2,4,3,1,0:T(8,128)} %copy.89), channel_id=1, source_target_pairs={{0,12},{1,13},{2,14},{3,15},{4,8},{5,9},{6,10},{7,11},{8,4},{9,5},... | collective-permute-start | bytes 983048 | tf_op jit(solution)/shard_map/ppermute | solution.py:88
  739.4 814.8 %collective-permute-start.14 = (f32[5,2,32,16,16]{2,4,3,1,0:T(8,128)}, f32[5,2,32,16,16]{2,4,3,1,0:T(8,128)}, u32[]{:S(2)}, u32[]{:S(2)}) collective-permute-start(f32[5,2,32,16,16]{2,4,3,1,0:T(8,128)} %copy.91), channel_id=1, source_target_pairs={{0,13},{1,12},{2,15},{3,14},{4,9},{5,8},{6,11},{7,10},{8,5},{9,4},... | collective-permute-start | bytes 983048 | tf_op jit(solution)/shard_map/ppermute | solution.py:88
  740.6 868.7 %collective-permute-start.15 = (f32[5,2,32,16,16]{2,4,3,1,0:T(8,128)}, f32[5,2,32,16,16]{2,4,3,1,0:T(8,128)}, u32[]{:S(2)}, u32[]{:S(2)}) collective-permute-start(f32[5,2,32,16,16]{2,4,3,1,0:T(8,128)} %copy.93), channel_id=1, source_target_pairs={{0,14},{1,15},{2,12},{3,13},{4,10},{5,11},{6,8},{7,9},{8,6},{9,7},... | collective-permute-start | bytes 983048 | tf_op jit(solution)/shard_map/ppermute | solution.py:88
  904.1 760.3 %collective-permute-start.16 = (f32[5,2,32,16,16]{2,4,3,1,0:T(8,128)}, f32[5,2,32,16,16]{2,4,3,1,0:T(8,128)}, u32[]{:S(2)}, u32[]{:S(2)}) collective-permute-start(f32[5,2,32,16,16]{2,4,3,1,0:T(8,128)} %copy.95), channel_id=1, source_target_pairs={{0,15},{1,14},{2,13},{3,12},{4,11},{5,10},{6,9},{7,8},{8,7},{9,6},... | collective-permute-start | bytes 983048 | tf_op jit(solution)/shard_map/ppermute | solution.py:88
  (3 other events, 13.6 us)
